TPU v7x, 32 devices: a whole 2x2x4 slice. The times are simulated.
32 devices in a mesh: gx: 8 (over y, x, core), gy: 4 (over z).
Axes of the slice: x: 2, y: 2, z: 4, core: 2. Of those that a mesh axis runs over, the one named last changes fastest.
Arguments:
- layer_early: bfloat16 [1024, 8192], P(None, ('gx', 'gy')), may hold values from -48 to 48
- layer_late: bfloat16 [1024, 8192], P(('gx', 'gy')), may hold values from -48 to 48
Outputs:
- similarity: float32 [], replicated
- token_share: float32 [1024], P(('gx', 'gy'))
- early_rows: bfloat16 [1024, 8192], P(('gx', 'gy'))
- late_rows: bfloat16 [1024, 8192], P(('gx', 'gy'))
All inputs are finite; a program needn't handle non-finite values.
Results may differ from a plain program's by a relative error of at most 0.0015.
Values may be sent and summed in bfloat16 or wider, within the bound.
A program may use at most 128 MiB of HBM per device.

v0:
```python
import jax
import jax.numpy as jnp
from jax import lax
from jax.sharding import PartitionSpec as P


def pair_terms(left_early, left_late, right_early, right_late):
    dims = (((1,), (1,)), ((), ()))
    block_early = lax.dot_general(left_early, right_early, dims, preferred_element_type=jnp.float32)
    block_late = lax.dot_general(left_late, right_late, dims, preferred_element_type=jnp.float32)
    return (
        jnp.sum(block_early * block_late, axis=1),
        jnp.sum(block_early * block_early),
        jnp.sum(block_late * block_late),
    )


def body(layer_early, layer_late):
    total_rows = layer_early.shape[0]
    early_values = layer_early.astype(jnp.float32)
    early_cols = (early_values - jnp.mean(early_values, axis=0)).astype(jnp.bfloat16)
    late_values = layer_late.astype(jnp.float32)
    column_sums = lax.psum(jnp.sum(late_values, axis=0), ("gx", "gy"))
    late_rows = (late_values - column_sums / total_rows).astype(jnp.bfloat16)
    early_rows = lax.all_to_all(early_cols, ("gx", "gy"), split_axis=0, concat_axis=1, tiled=True)
    block_early, block_late = (
        lax.all_gather(early_rows, "gy", axis=0, tiled=True),
        lax.all_gather(late_rows, "gy", axis=0, tiled=True),
    )
    row_part, early_part, late_part = pair_terms(
        block_early,
        block_late,
        lax.all_gather(early_rows, "gx", axis=0, tiled=True),
        lax.all_gather(late_rows, "gx", axis=0, tiled=True),
    )
    own_align = lax.psum_scatter(row_part, "gy", scatter_dimension=0, tiled=True)
    total_kl, total_kk, total_ll = lax.psum(
        (jnp.sum(row_part), early_part, late_part), ("gx", "gy")
    )
    scale_norm = jnp.sqrt(total_kk * total_ll)
    similarity = total_kl / scale_norm
    token_share = total_rows * own_align / scale_norm
    return (similarity, token_share, early_rows, late_rows)


def solution(mesh):
    in_specs = (P(None, ("gx", "gy")), P(("gx", "gy"), None))
    out_specs = (P(), P(("gx", "gy")), P(("gx", "gy"), None), P(("gx", "gy"), None))
    return jax.shard_map(body, mesh=mesh, in_specs=in_specs, out_specs=out_specs, check_vma=False)
```

profile of v0, /device:TPU:0, one launch (start us, length us, event | category | flops | bytes accessed | tf_op | source)
XLA Modules:
  0.0 298.2 jit_solution(8457581897998979989)
XLA Ops:
  7.2 0.0 copy-start
  7.2 0.0 all-gather.9.cloned.1.call-start
  7.2 1.2 convert_reduce_fusion
  8.4 42.1 %psum.28 = f32[8192]{0:T(1024)S(1)} all-reduce(f32[8192]{0:T(1024)S(1)} %convert_reduce_fusion), channel_id=1, replica_groups=mesh['gx'=8,'gy'=4] {'gx','gy'}, use_global_device_ids=true, to_apply=%region_2.0 | all-reduce | flops 8192 | bytes 65536 | tf_op jit(solution)/shard_map/psum | solution.py:23
  50.6 1.9 fusion.1
  52.5 0.0 all-gather.9.cloned.1.call-update
  52.5 0.0 all-gather.11.cloned.1.call-start
  52.5 0.7 all-gather.11.cloned.1.call-update
  53.3 0.0 all-gather.5.cloned.1.call-start
  53.3 1.2 convert_reduce_fusion.1
  54.5 1.1 fusion
  55.6 28.2 %all_to_all.19 = bf16[32,32,256]{2,1,0:T(8,128)(2,1)S(1)} all-to-all(bf16[32,32,256]{2,1,0:T(8,128)(2,1)S(1)} %bitcast.12), channel_id=1, replica_groups=mesh['gx'=8,'gy'=4] {'gx','gy'}, dimensions={0} | all-to-all | bytes 1048576 | tf_op jit(solution)/shard_map/all_to_all | solution.py:25
  83.9 0.8 copy.8
  84.7 0.0 all-gather.5.cloned.1.call-update
  84.7 0.0 all-gather.7.cloned.1.call-start
  84.8 0.5 all-gather.7.cloned.1.call-update
  85.3 0.0 copy-done
  85.3 0.6 dynamic-slice
  86.6 22.4 %all-gather.9.cloned.1.call-done = bf16[128,8192]{1,0:T(8,128)(2,1)} async-done(((bf16[32,8192]{1,0:T(8,128)(2,1)}), bf16[128,8192]{1,0:T(8,128)(2,1)}) %all-gather.9.cloned.1.call-update) | async-done | bytes 2097168 | tf_op jit(solution)/shard_map/all_gather | solution.py:28
  109.0 38.1 %all-gather.11.cloned.1.call-done = bf16[256,8192]{1,0:T(8,128)(2,1)} async-done(((bf16[32,8192]{1,0:T(8,128)(2,1)}), bf16[256,8192]{1,0:T(8,128)(2,1)}) %all-gather.11.cloned.1.call-update) | async-done | bytes 4194320 | tf_op jit(solution)/shard_map/all_gather | solution.py:34
  147.1 4.4 %fusion.3 = f32[128,256]{1,0:T(8,128)S(1)} fusion(bf16[128,8192]{1,0:T(8,128)(2,1)} %all-gather.9.cloned.1.call-done, bf16[256,8192]{1,0:T(8,128)(2,1)} %all-gather.11.cloned.1.call-done), kind=kOutput, calls=%fused_computation.14 | convolution fusion | flops 536870912 | bytes 6422528 | tf_op jit(solution)/shard_map/dot_general | solution.py:10
  151.5 43.5 %all-gather.5.cloned.1.call-done = bf16[128,8192]{1,0:T(8,128)(2,1)} async-done(((bf16[32,8192]{1,0:T(8,128)(2,1)}), bf16[128,8192]{1,0:T(8,128)(2,1)}) %all-gather.5.cloned.1.call-update) | async-done | bytes 2097168 | tf_op jit(solution)/shard_map/all_gather | solution.py:27
  195.0 37.7 %all-gather.7.cloned.1.call-done = bf16[256,8192]{1,0:T(8,128)(2,1)} async-done(((bf16[32,8192]{1,0:T(8,128)(2,1)}), bf16[256,8192]{1,0:T(8,128)(2,1)}) %all-gather.7.cloned.1.call-update) | async-done | bytes 4194320 | tf_op jit(solution)/shard_map/all_gather | solution.py:33
  232.7 5.0 %multiply_reduce_fusion.2 = (f32[128]{0:T(128)S(1)}, f32[]{:T(128)}, f32[]{:T(128)}, f32[]{:T(128)}) fusion(f32[128,256]{1,0:T(8,128)S(1)} %fusion.3, bf16[128,8192]{1,0:T(8,128)(2,1)} %all-gather.5.cloned.1.call-done, bf16[256,8192]{1,0:T(8,128)(2,1)} %all-gather.7.cloned.1.call-done), kind=kOutput, calls=%fused_computation.8 | convolution fusion | flops 537100160 | bytes 6423052 | tf_op jit(solution)/shard_map/dot_general | solution.py:9
  237.7 39.6 %all-reduce.1 = (f32[]{:T(128)}, f32[]{:T(128)}, f32[]{:T(128)}) all-reduce(f32[]{:T(128)} %get-tuple-element.5, f32[]{:T(128)} %get-tuple-element.7, f32[]{:T(128)} %get-tuple-element.6), channel_id=1, replica_groups=mesh['gx'=8,'gy'=4] {'gx','gy'}, use_global_device_ids=true, to_apply=%region_4.0 | all-reduce | flops 3 | bytes 24 | tf_op jit(solution)/shard_map/psum | solution.py:37
  278.7 10.6 %all-reduce = f32[128]{0:T(128)S(1)} all-reduce(f32[128]{0:T(128)S(1)} %get-tuple-element.4), channel_id=2, replica_groups=mesh['gx'=8,'gy'=4] {'gy'}, use_global_device_ids=true, to_apply=%region_10.0.clone | all-reduce | flops 128 | bytes 1024
  290.0 0.6 fusion.2
  (2 shorter events, 0.0 us)
Async XLA Ops:
  7.2 78.2 %copy-start = (u32[32]{0:T(128)S(1)}, u32[32]{0:T(128)}, u32[]{:S(2)}) copy-start(u32[32]{0:T(128)} %constant.11) | copy-start | bytes 388
  7.2 101.8 %all-gather.9.cloned.1.call-start = ((), (), s32[]{:S(2)}) async-start(), calls=%async_computation.3 | async-start | bytes 2621440 | tf_op jit(solution)/shard_map/all_gather | solution.py:28
  52.5 94.6 %all-gather.11.cloned.1.call-start = ((), (), s32[]{:S(2)}) async-start(), calls=%async_computation.4 | async-start | bytes 4718592 | tf_op jit(solution)/shard_map/all_gather | solution.py:34
  53.3 141.7 %all-gather.5.cloned.1.call-start = ((), (), s32[]{:S(2)}) async-start(), calls=%async_computation.1 | async-start | bytes 2621440 | tf_op jit(solution)/shard_map/all_gather | solution.py:27
  84.7 147.9 %all-gather.7.cloned.1.call-start = ((), (), s32[]{:S(2)}) async-start(), calls=%async_computation.2 | async-start | bytes 4718592 | tf_op jit(solution)/shard_map/all_gather | solution.py:33
Sparse Core Ops, SparseCore 0:
  52.6 56.3 all-gather.8
  111.5 35.5 all-gather.10
  149.3 45.6 all-gather.4
  197.3 35.3 all-gather.6
where the time goes:
time: 299 us; the launch traced here: 298 us
  waiting for transfers between devices  143 us (48%)
  blocking collectives  121 us (40%)
  between operations  17.6 us (6%)
  matrix products  9.4 us (3%)
  other arithmetic  6.03 us (2%)
    all_gather x1, waiting for transfers between devices, body(): lax.all_gather(early_rows, 'gy', axis=0, tiled=True)  43.5 us
    psum x1, blocking collectives, body(): column_sums = lax.psum(jnp.sum(late_values, axis=0), ('gx', 'gy'))  42.1 us
    psum x1, blocking collectives, body(): lax.psum((jnp.sum(row_part), early_part, late_part), ('gx', 'gy'))  39.6 us
    all_gather x1, waiting for transfers between devices, body(): lax.all_gather(late_rows, 'gx', axis=0, tiled=True)  38.1 us
    all_gather x1, waiting for transfers between devices, body(): lax.all_gather(early_rows, 'gx', axis=0, tiled=True)  37.7 us
    all_to_all x1, blocking collectives, body(): lax.all_to_all(early_cols, ('gx', 'gy'), split_axis=0, concat_axis=1, til...  28.2 us
    all_gather x1, waiting for transfers between devices, body(): lax.all_gather(late_rows, 'gy', axis=0, tiled=True)  22.4 us
    unnamed x1, blocking collectives  10.6 us
  transfers between devices with their start and end apart: 4, of which 4 were waited for; matrix products, arithmetic and copies ran while one was open for 3% of the time, Pallas kernels for 0%

commit v1 on v0

--- a/solution.py
+++ b/solution.py
@@ -22,7 +22,15 @@
     late_values = layer_late.astype(jnp.float32)
     column_sums = lax.psum(jnp.sum(late_values, axis=0), ("gx", "gy"))
     late_rows = (late_values - column_sums / total_rows).astype(jnp.bfloat16)
-    early_rows = lax.all_to_all(early_cols, ("gx", "gy"), split_axis=0, concat_axis=1, tiled=True)
+    early_rows = jnp.concatenate(
+        lax.all_to_all(
+            jnp.stack(jnp.split(early_cols, lax.axis_size(("gx", "gy")), axis=0)),
+            ("gx", "gy"),
+            0,
+            0,
+        ),
+        axis=1,
+    )
     block_early, block_late = (
         lax.all_gather(early_rows, "gy", axis=0, tiled=True),
         lax.all_gather(late_rows, "gy", axis=0, tiled=True),

time: 299 us -> 299 us (level)
  waiting for transfers between devices: 143 us -> 140 us
where the time goes in v1:
time: 299 us; the launch traced here: 298 us
  waiting for transfers between devices  140 us (47%)
  blocking collectives  123 us (41%)
  between operations  17.9 us (6%)
  matrix products  9.4 us (3%)
  other arithmetic  6.03 us (2%)
    all_gather x1, waiting for transfers between devices, body(): lax.all_gather(early_rows, 'gy', axis=0, tiled=True)  43.5 us
    psum x1, blocking collectives, body(): column_sums = lax.psum(jnp.sum(late_values, axis=0), ('gx', 'gy'))  42.1 us
    psum x1, blocking collectives, body(): lax.psum((jnp.sum(row_part), early_part, late_part), ('gx', 'gy'))  39.6 us
    all_gather x1, waiting for transfers between devices, body(): lax.all_gather(late_rows, 'gx', axis=0, tiled=True)  37.8 us
    all_gather x1, waiting for transfers between devices, body(): lax.all_gather(early_rows, 'gx', axis=0, tiled=True)  37.7 us
    all_to_all x1, blocking collectives, body(): lax.all_to_all(jnp.stack(jnp.split(early_cols, lax.axis_size(('gx', 'gy')...  30.6 us
    all_gather x1, waiting for transfers between devices, body(): lax.all_gather(late_rows, 'gy', axis=0, tiled=True)  20.1 us
    unnamed x1, blocking collectives  10.6 us
  transfers between devices with their start and end apart: 4, of which 4 were waited for; matrix products, arithmetic and copies ran while one was open for 3% of the time, Pallas kernels for 0%

profile of v1, /device:TPU:0, one launch (start us, length us, event | category | flops | bytes accessed | tf_op | source)
XLA Modules:
  0.0 298.3 jit_solution(7248487822186111369)
XLA Ops:
  7.2 0.0 copy-start
  7.2 0.0 all-gather.9.cloned.1.call-start
  7.2 1.2 convert_reduce_fusion
  8.4 42.1 %psum.28 = f32[8192]{0:T(1024)S(1)} all-reduce(f32[8192]{0:T(1024)S(1)} %convert_reduce_fusion), channel_id=1, replica_groups=mesh['gx'=8,'gy'=4] {'gx','gy'}, use_global_device_ids=true, to_apply=%region_2.0 | all-reduce | flops 8192 | bytes 65536 | tf_op jit(solution)/shard_map/psum | solution.py:23
  50.6 1.9 fusion.1
  52.5 0.0 all-gather.9.cloned.1.call-update
  52.5 0.0 all-gather.11.cloned.1.call-start
  52.5 0.7 all-gather.11.cloned.1.call-update
  53.3 0.0 all-gather.5.cloned.1.call-start
  53.3 1.2 convert_reduce_fusion.1
  54.5 1.1 fusion
  56.0 30.6 %all_to_all.5 = bf16[32,32,256]{2,1,0:T(8,128)(2,1)S(1)} all-to-all(bf16[32,32,256]{2,1,0:T(8,128)(2,1)S(1)} %constant_dynamic-update-slice_fusion), channel_id=1, replica_groups=mesh['gx'=8,'gy'=4] {'gx','gy'}, dimensions={0} | all-to-all | bytes 1048576 | tf_op jit(solution)/shard_map/all_to_all | solution.py:26
  86.6 0.8 copy.8
  87.4 0.0 all-gather.5.cloned.1.call-update
  87.4 0.0 all-gather.7.cloned.1.call-start
  87.5 0.5 all-gather.7.cloned.1.call-update
  88.0 0.0 copy-done
  88.0 0.6 dynamic-slice
  89.3 20.1 %all-gather.9.cloned.1.call-done = bf16[128,8192]{1,0:T(8,128)(2,1)} async-done(((bf16[32,8192]{1,0:T(8,128)(2,1)}), bf16[128,8192]{1,0:T(8,128)(2,1)}) %all-gather.9.cloned.1.call-update) | async-done | bytes 2097168 | tf_op jit(solution)/shard_map/all_gather | solution.py:36
  109.4 37.8 %all-gather.11.cloned.1.call-done = bf16[256,8192]{1,0:T(8,128)(2,1)} async-done(((bf16[32,8192]{1,0:T(8,128)(2,1)}), bf16[256,8192]{1,0:T(8,128)(2,1)}) %all-gather.11.cloned.1.call-update) | async-done | bytes 4194320 | tf_op jit(solution)/shard_map/all_gather | solution.py:42
  147.2 4.4 %fusion.3 = f32[128,256]{1,0:T(8,128)S(1)} fusion(bf16[128,8192]{1,0:T(8,128)(2,1)} %all-gather.9.cloned.1.call-done, bf16[256,8192]{1,0:T(8,128)(2,1)} %all-gather.11.cloned.1.call-done), kind=kOutput, calls=%fused_computation.78 | convolution fusion | flops 536870912 | bytes 6422528 | tf_op jit(solution)/shard_map/dot_general | solution.py:10
  151.6 43.5 %all-gather.5.cloned.1.call-done = bf16[128,8192]{1,0:T(8,128)(2,1)} async-done(((bf16[32,8192]{1,0:T(8,128)(2,1)}), bf16[128,8192]{1,0:T(8,128)(2,1)}) %all-gather.5.cloned.1.call-update) | async-done | bytes 2097168 | tf_op jit(solution)/shard_map/all_gather | solution.py:35
  195.1 37.7 %all-gather.7.cloned.1.call-done = bf16[256,8192]{1,0:T(8,128)(2,1)} async-done(((bf16[32,8192]{1,0:T(8,128)(2,1)}), bf16[256,8192]{1,0:T(8,128)(2,1)}) %all-gather.7.cloned.1.call-update) | async-done | bytes 4194320 | tf_op jit(solution)/shard_map/all_gather | solution.py:41
  232.8 5.0 %multiply_reduce_fusion.2 = (f32[128]{0:T(128)S(1)}, f32[]{:T(128)}, f32[]{:T(128)}, f32[]{:T(128)}) fusion(f32[128,256]{1,0:T(8,128)S(1)} %fusion.3, bf16[128,8192]{1,0:T(8,128)(2,1)} %all-gather.5.cloned.1.call-done, bf16[256,8192]{1,0:T(8,128)(2,1)} %all-gather.7.cloned.1.call-done), kind=kOutput, calls=%fused_computation.40 | convolution fusion | flops 537100160 | bytes 6423052 | tf_op jit(solution)/shard_map/dot_general | solution.py:9
  237.8 39.6 %all-reduce.1 = (f32[]{:T(128)}, f32[]{:T(128)}, f32[]{:T(128)}) all-reduce(f32[]{:T(128)} %get-tuple-element.5, f32[]{:T(128)} %get-tuple-element.7, f32[]{:T(128)} %get-tuple-element.6), channel_id=1, replica_groups=mesh['gx'=8,'gy'=4] {'gx','gy'}, use_global_device_ids=true, to_apply=%region_4.0 | all-reduce | flops 3 | bytes 24 | tf_op jit(solution)/shard_map/psum | solution.py:45
  278.8 10.6 %all-reduce = f32[128]{0:T(128)S(1)} all-reduce(f32[128]{0:T(128)S(1)} %get-tuple-element.4), channel_id=2, replica_groups=mesh['gx'=8,'gy'=4] {'gy'}, use_global_device_ids=true, to_apply=%region_10.0.clone | all-reduce | flops 128 | bytes 1024
  290.1 0.6 fusion.2
  (34 shorter events, 0.1 us)
Async XLA Ops:
  7.2 80.9 %copy-start = (u32[32]{0:T(128)S(1)}, u32[32]{0:T(128)}, u32[]{:S(2)}) copy-start(u32[32]{0:T(128)} %constant.11) | copy-start | bytes 388
  7.2 102.2 %all-gather.9.cloned.1.call-start = ((), (), s32[]{:S(2)}) async-start(), calls=%async_computation.3 | async-start | bytes 2621440 | tf_op jit(solution)/shard_map/all_gather | solution.py:36
  52.5 94.7 %all-gather.11.cloned.1.call-start = ((), (), s32[]{:S(2)}) async-start(), calls=%async_computation.4 | async-start | bytes 4718592 | tf_op jit(solution)/shard_map/all_gather | solution.py:42
  53.3 141.8 %all-gather.5.cloned.1.call-start = ((), (), s32[]{:S(2)}) async-start(), calls=%async_computation.1 | async-start | bytes 2621440 | tf_op jit(solution)/shard_map/all_gather | solution.py:35
  87.4 145.4 %all-gather.7.cloned.1.call-start = ((), (), s32[]{:S(2)}) async-start(), calls=%async_computation.2 | async-start | bytes 4718592 | tf_op jit(solution)/shard_map/all_gather | solution.py:41
Sparse Core Ops, SparseCore 0:
  52.6 56.7 all-gather.8
  111.8 35.3 all-gather.10
  149.4 45.6 all-gather.4
  197.4 35.3 all-gather.6
